TPU v7x, 128 devices: a whole 4x4x4 slice. The times are simulated.
128 devices in a mesh: teach: 2 (over core), dp: 64 (over x, z, y).
Axes of the slice: x: 4, y: 4, z: 4, core: 2. Of those that a mesh axis runs over, the one named last changes fastest.
Arguments:
- teacher_logits: bfloat16 [2, 16384, 5000], P('teach', 'dp'), may hold values from -18 to 400
- routes: int32 [16384, 1], P('dp'), may hold values from 0 to 127; in each aligned block of 256 rows (0 to 255, 256 to 511, ...) at most 4 rows name the same one
- agreement: int32 [16384], P('dp'), may hold values 0 or 1
- targets: int32 [16384], P('dp'), may hold values from 0 to 4999
- lengths: int32 [64], P('dp'), may hold values from 64 to 256
- student_hidden: bfloat16 [32768, 1024], P(('teach', 'dp')), may hold values from -6 to 6
- out_weight: bfloat16 [1024, 5000], replicated, may hold values from -2 to 2
- out_bias: float32 [5000], replicated, may hold values from -6 to 6
- gain: float32 [1024], replicated, may hold values from 0.5 to 1.5
Outputs:
- weight_grad: float32 [1024, 5000], P(('teach', 'dp'))
- gain_grad: float32 [1024], replicated
- bias_grad: float32 [5000], replicated
- loss: float32 [], replicated
Inputs may be any that keep to these rules, and one draw needn't show every extreme that they name: `routes`: within the 256 rows of one index of dp, each student device is named at most 4 times, and some device exactly 4 times.
All inputs are finite; a program needn't handle non-finite values. No bound on the sum of `agreement` on one device may be relied on, other than what follows from the above.
Results may differ from a plain program's by a relative error of at most 0.0031.
Values may be sent and summed in bfloat16 or wider, within the bound.
A program may use at most 128 MiB of HBM per device.

v0:
```python
import jax
import jax.numpy as jnp
from jax import lax
from jax.sharding import Mesh
from jax.sharding import PartitionSpec as P

LMAX = 256
DP = ("dp_0", "dp_1", "dp_2")
TEACH_DP = ("teach", "dp_0", "dp_1", "dp_2")
EPSILON = 1e-05


def over_axes(x, axes):
    for axis in axes:
        x = lax.psum(x, axis)
    return x


def route_slots(dest_device, devices):
    onehot = (dest_device[:, None] == jnp.arange(devices, dtype=jnp.int32)[None, :]).astype(
        jnp.float32
    )
    row_ids = jnp.arange(dest_device.shape[0], dtype=jnp.int32)
    earlier = (row_ids[None, :] < row_ids[:, None]).astype(jnp.float32)
    before = jnp.dot(
        earlier, onehot, preferred_element_type=jnp.float32, precision=lax.Precision.HIGHEST
    )
    return jnp.sum(before * onehot, axis=1).astype(jnp.int32)


def live_mask(lengths_block, row_total):
    row_ids = jnp.arange(row_total, dtype=jnp.int32)
    utterance = row_ids // LMAX
    frame_pos = row_ids % LMAX
    picks = utterance[:, None] == jnp.arange(lengths_block.shape[0], dtype=jnp.int32)[None, :]
    row_length = jnp.sum(jnp.where(picks, lengths_block[None, :], 0), axis=1)
    return (frame_pos < row_length).astype(jnp.float32)


def soft_targets(teacher_rows, agree_rows, target_rows, live_rows):
    probs_teacher = jax.nn.softmax(teacher_rows.astype(jnp.float32), axis=-1)
    onehot = (
        target_rows[:, None] == jnp.arange(probs_teacher.shape[1], dtype=jnp.int32)[None, :]
    ).astype(jnp.float32)
    weight = (0.5 * agree_rows.astype(jnp.float32))[:, None]
    return (live_rows[:, None] * (weight * probs_teacher + 0.5 * onehot)).astype(jnp.bfloat16)


def student_forward(hidden_rows, gain, out_weight, out_bias):
    states = hidden_rows.astype(jnp.float32)
    centre = jnp.mean(states, axis=1, keepdims=True)
    spread = jnp.mean(jnp.square(states - centre), axis=1, keepdims=True)
    normed = (states - centre) * lax.rsqrt(spread + EPSILON)
    scaled = (normed * gain[None, :]).astype(jnp.bfloat16)
    logits = jnp.dot(scaled, out_weight, preferred_element_type=jnp.float32) + out_bias[None, :]
    return (normed, scaled, jax.nn.log_softmax(logits, axis=-1))


def combined_grads(first_soft, second_soft, log_probs):
    first_float = first_soft.astype(jnp.float32)
    second_float = second_soft.astype(jnp.float32)
    row_mass = jnp.sum(first_float + second_float, axis=1, keepdims=True)
    return (row_mass * jnp.exp(log_probs) - first_float - second_float).astype(jnp.bfloat16)


def body(
    teacher_logits, routes, agreement, targets, lengths, student_hidden, out_weight, out_bias, gain
):
    teach_count = lax.axis_size("teach")
    data_count = lax.axis_size(DP)
    devices = teach_count * data_count
    rows_here = teacher_logits.shape[1]
    most_slots = 2 * rows_here // devices
    vocab = teacher_logits.shape[2]
    width = student_hidden.shape[1]
    dest_device = routes[:, 0]
    slot_index = route_slots(dest_device, devices)
    live_rows = live_mask(lengths, rows_here)
    soft_rows = soft_targets(teacher_logits[0], agreement, targets, live_rows)
    half = rows_here // 2
    first_here = lax.axis_index("teach") * half
    count_term = jnp.sum(lax.dynamic_slice_in_dim(live_rows, first_here, half, 0))
    stacked = soft_rows.reshape(2, half, vocab)
    both_soft = lax.all_to_all(stacked, "teach", split_axis=0, concat_axis=0, tiled=True)
    dest_half = lax.dynamic_slice_in_dim(dest_device, first_here, half, 0)
    slot_half = lax.dynamic_slice_in_dim(slot_index, first_here, half, 0)
    replicated = jnp.broadcast_to(
        student_hidden.reshape(1, data_count, most_slots, width),
        (teach_count, data_count, most_slots, width),
    ).reshape(devices, most_slots, width)
    arrived = lax.all_to_all(replicated, TEACH_DP, split_axis=0, concat_axis=0, tiled=True)
    hidden_rows = arrived[dest_half, slot_half]
    norm_rows, state_rows, log_probs = student_forward(hidden_rows, gain, out_weight, out_bias)
    grad_rows = combined_grads(both_soft[0], both_soft[1], log_probs)
    loss_term = -jnp.sum(
        (both_soft[0].astype(jnp.float32) + both_soft[1].astype(jnp.float32)) * log_probs
    )
    back_rows = lax.dot_general(
        grad_rows, out_weight, (((1,), (1,)), ((), ())), preferred_element_type=jnp.float32
    )
    gain_grad = jnp.sum(back_rows * norm_rows, axis=0)
    bias_grad = jnp.sum(grad_rows.astype(jnp.float32), axis=0)
    weight_grad = lax.psum_scatter(
        lax.dot_general(
            state_rows, grad_rows, (((0,), (0,)), ((), ())), preferred_element_type=jnp.float32
        ),
        TEACH_DP,
        scatter_dimension=0,
        tiled=True,
    )
    gain_sum, bias_sum, loss_sum, total_frames = (
        over_axes(gain_grad, TEACH_DP),
        over_axes(bias_grad, TEACH_DP),
        over_axes(loss_term, TEACH_DP),
        over_axes(count_term, TEACH_DP),
    )
    inverse = 1.0 / total_frames
    return (weight_grad * inverse, gain_sum * inverse, bias_sum * inverse, loss_sum * inverse)


def solution(mesh):
    finer = Mesh(
        mesh.devices.reshape(mesh.shape["teach"], 4, 4, 4), ("teach", "dp_0", "dp_1", "dp_2")
    )
    in_specs = (
        P("teach", DP, None),
        P(DP, None),
        P(DP),
        P(DP),
        P(DP),
        P(TEACH_DP, None),
        P(),
        P(),
        P(),
    )
    out_specs = (P(TEACH_DP, None), P(), P(), P())
    return jax.shard_map(body, mesh=finer, in_specs=in_specs, out_specs=out_specs, check_vma=False)
```

profile of v0, /device:TPU:1, one launch (start us, length us, event | category | flops | bytes accessed | tf_op | source)
XLA Modules:
  0.0 780.8 jit_solution(15204521626412033606)
XLA Ops:
  7.2 0.0 copy-start
  7.2 1.4 broadcast_in_dim.22
  8.6 1.2 broadcast_in_dim.23
  9.8 11.9 %all-to-all-start = ((bf16[128,4,1024]{2,1,0:T(4,128)(2,1)}), bf16[128,4,1024]{2,1,0:T(4,128)(2,1)}, u32[]{:S(2)}, u32[]{:S(2)}) async-start(bf16[128,4,1024]{2,1,0:T(4,128)(2,1)} %bitcast.51), calls=%async_computation | async-start | bytes 2097152 | tf_op jit(solution)/shard_map/all_to_all | solution.py:91
  22.4 0.0 copy-done
  22.4 4.0 copy.13
  26.4 0.0 copy-start.6
  26.4 0.0 copy-start.7
  26.4 0.7 reduce_max.28
  27.1 0.0 copy-done.6
  27.1 0.0 copy-done.7
  27.1 0.2 fusion.5
  27.4 0.9 fusion.1
  28.3 0.0 copy-start.5
  28.3 5.9 copy.14
  34.2 0.1 fusion.18
  34.3 0.0 copy-done.5
  34.3 5.7 multiply_convert_fusion
  40.0 0.0 all-to-all-done
  40.0 6.1 all-to-all-start.1
  46.1 0.0 copy-start.3
  46.1 0.0 copy-start.4
  46.1 0.0 reduce-scatter.2.cloned.1.call-start
  46.1 2.3 gather_fusion
  48.4 0.1 convert_reduce_fusion.1
  48.5 0.2 fusion.10
  48.8 0.0 copy-done.3
  48.8 0.0 copy-done.4
  48.8 6.3 fusion.23
  55.1 0.7 exponential_reduce_fusion
  55.8 0.0 all-to-all-done.1
  55.8 3.0 multiply_reduce_fusion
  58.8 2.7 convert_reduce_fusion
  61.5 0.0 copy-start.1
  61.5 1.0 copy-done.1
  62.5 8.7 %fusion.19 = f32[1024,5000]{1,0:T(8,128)} fusion(bf16[128,5000]{0,1:T(8,128)(2,1)S(1)} %get-tuple-element.23, bf16[128,1024]{1,0:T(8,128)(2,1)S(1)} %gather_fusion, f32[1024]{0:T(1024)S(1)} %copy-done.3, f32[128]{0:T(128)S(1)} %add_rsqrt_fusion, f32[128]{0:T(128)S(1)} %broadcast_multiply_fusion.3), kind=kOutput, calls=%fused_computation.58 | convolution fusion | flops 1311375360 | bytes 22027264 | tf_op jit(solution)/shard_map/dot_general | solution.py:104
  71.2 0.0 reduce-scatter.2.cloned.1.call-update
  71.2 0.7 dynamic-slice_reduce_fusion
  72.6 0.0 copy-done.2
  72.6 5.6 fusion.4
  78.2 4.5 all-reduce.3
  82.8 14.6 %all-reduce.2 = (f32[]{:T(128)}, f32[1024]{0:T(1024)S(1)}, f32[5000]{0:T(1024)S(1)}, f32[]{:T(128)}) all-reduce(f32[]{:T(128)} %get-tuple-element.18, f32[1024]{0:T(1024)S(1)} %get-tuple-element.19, f32[5000]{0:T(1024)S(1)} %get-tuple-element.20, f32[]{:T(128)} %get-tuple-element.21), channel_id=1, replica_groups=mesh['teach'=2,'dp_0'=4,'dp_1'=4,'dp_2'=4] {'dp_0'}, use_global_device_ids=true, to_apply=%region_11.12 | all-reduce | flops 6026 | bytes 48208 | tf_op jit(solution)/shard_map/psum | solution.py:15
  97.3 16.6 %all-reduce.1 = (f32[]{:T(128)}, f32[1024]{0:T(1024)S(1)}, f32[5000]{0:T(1024)S(1)}, f32[]{:T(128)}) all-reduce(f32[]{:T(128)} %get-tuple-element.14, f32[1024]{0:T(1024)S(1)} %get-tuple-element.15, f32[5000]{0:T(1024)S(1)} %get-tuple-element.16, f32[]{:T(128)} %get-tuple-element.17), channel_id=1, replica_groups=mesh['teach'=2,'dp_0'=4,'dp_1'=4,'dp_2'=4] {'dp_1'}, use_global_device_ids=true, to_apply=%region_12.13 | all-reduce | flops 6026 | bytes 48208 | tf_op jit(solution)/shard_map/psum | solution.py:15
  114.0 15.5 %all-reduce = (f32[]{:T(128)}, f32[1024]{0:T(1024)S(1)}, f32[5000]{0:T(1024)S(1)}, f32[]{:T(128)}) all-reduce(f32[]{:T(128)} %get-tuple-element.10, f32[1024]{0:T(1024)S(1)} %get-tuple-element.11, f32[5000]{0:T(1024)S(1)} %get-tuple-element.12, f32[]{:T(128)} %get-tuple-element.13), channel_id=1, replica_groups=mesh['teach'=2,'dp_0'=4,'dp_1'=4,'dp_2'=4] {'dp_2'}, use_global_device_ids=true, to_apply=%region_13.14 | all-reduce | flops 6026 | bytes 48208 | tf_op jit(solution)/shard_map/psum | solution.py:15
  130.8 0.6 broadcast_multiply_fusion.2
  131.4 0.6 broadcast_multiply_fusion.1
  132.0 639.2 %reduce-scatter.2.cloned.1.call-done = f32[8,5000]{1,0:T(8,128)} async-done(((f32[1024,5000]{1,0:T(8,128)}), f32[8,5000]{1,0:T(8,128)}) %reduce-scatter.2.cloned.1.call-update) | async-done | bytes 160016 | tf_op jit(solution)/shard_map/reduce_scatter | solution.py:103
  771.2 1.6 broadcast_multiply_fusion
  (9 shorter events, 0.1 us)
Async XLA Ops:
  7.2 15.3 %copy-start = (bf16[1,256,5000]{1,2,0:T(8,128)(2,1)S(1)}, bf16[1,256,5000]{1,2,0:T(8,128)(2,1)}, u32[]{:S(2)}) copy-start(bf16[1,256,5000]{1,2,0:T(8,128)(2,1)} %param.9) | copy-start | bytes 7680004
  9.8 30.2 %all-to-all-start = ((bf16[128,4,1024]{2,1,0:T(4,128)(2,1)}), bf16[128,4,1024]{2,1,0:T(4,128)(2,1)}, u32[]{:S(2)}, u32[]{:S(2)}) async-start(bf16[128,4,1024]{2,1,0:T(4,128)(2,1)} %bitcast.51), calls=%async_computation | async-start | bytes 2097152 | tf_op jit(solution)/shard_map/all_to_all | solution.py:91
  26.4 0.7 copy-start.6
  26.4 0.7 copy-start.7
  28.3 6.0 copy-start.5
  40.0 15.8 %all-to-all-start.1 = ((bf16[2,128,5000]{1,2,0:T(8,128)(2,1)}), bf16[2,128,5000]{1,2,0:T(8,128)(2,1)}, u32[]{:S(2)}, u32[]{:S(2)}) async-start(bf16[2,128,5000]{1,2,0:T(8,128)(2,1)} %multiply_convert_fusion), calls=%async_computation.1 | async-start | bytes 5120000 | tf_op jit(solution)/shard_map/all_to_all | solution.py:84
  46.1 2.7 copy-start.3
  46.1 2.7 copy-start.4
  46.1 725.1 %reduce-scatter.2.cloned.1.call-start = ((), (), s32[]{:S(2)}) async-start(), calls=%async_computation.3 | async-start | bytes 21135360 | tf_op jit(solution)/shard_map/reduce_scatter | solution.py:103
  61.5 1.0 copy-start.1
  71.2 1.4 copy-start.2
Sparse Core Ops, SparseCore 0:
  71.3 699.7 reduce-scatter.1
where the time goes:
time: 781 us
  waiting for transfers between devices  639 us (82%)
  blocking collectives  51.3 us (7%)
  matrix products  20.9 us (3%)
  starting transfers between devices  18.1 us (2%)
  between operations  17.9 us (2%)
  other arithmetic  17.5 us (2%)
  local copies, waits for them, and re-layouts  15.9 us (2%)
    reduce_scatter x1, waiting for transfers between devices, body(): lax.psum_scatter(lax.dot_general(state_rows, grad_rows, (((0,), (0,)), ((...  639 us
    psum x4, blocking collectives, over_axes(): x = lax.psum(x, axis)  51.3 us
  transfers between devices with their start and end apart: 3, of which 1 were waited for; matrix products, arithmetic and copies ran while one was open for 4% of the time, Pallas kernels for 0%

commit v1 on v0

--- a/solution.py
+++ b/solution.py
@@ -12,7 +12,8 @@
 
 def over_axes(x, axes):
     for axis in axes:
-        x = lax.psum(x, axis)
+        pieces = lax.all_gather(x, axis)
+        x = jnp.sum(pieces, axis=0)
     return x
 
 

time: 781 us -> 885 us (1.13)
  waiting for transfers between devices: 639 us -> 696 us
  local copies, waits for them, and re-layouts: 15.9 us -> 34.5 us
  blocking collectives: 51.3 us -> 68.3 us
    unnamed x1 -> x7, waiting for transfers between devices: 0.02 us -> 78.8 us
    psum x4 -> x0, blocking collectives: 51.3 us -> none  [over_axes(): x = lax.psum(x, axis)]
    all_gather x0 -> x4, blocking collectives: none -> 38.9 us  [over_axes(): pieces = lax.all_gather(x, axis)]
    unnamed x0 -> x4, blocking collectives: none -> 29.4 us
    reduce_scatter x1, waiting for transfers between devices: 639 us -> 617 us  [body(): lax.psum_scatter(lax.dot_general(state_rows, grad_rows, (((0,), (0,)), ((...]
    unnamed x16 -> x56, local copies, waits for them, and re-layouts: 1.06 us -> 16.6 us
  transfers between devices with their start and end apart: 3 -> 6, of which waited for: 1 -> 3; matrix products, arithmetic and copies ran while one was open for 4% -> 7% of each run, Pallas kernels for 0% -> 0%
where the time goes in v1:
time: 885 us; the launch traced here: 884 us
  waiting for transfers between devices  696 us (79%)
  blocking collectives  68.3 us (8%)
  local copies, waits for them, and re-layouts  34.5 us (4%)
  other arithmetic  23.6 us (3%)
  matrix products  22.2 us (3%)
  between operations  21.9 us (2%)
  starting transfers between devices  18.2 us (2%)
    reduce_scatter x1, waiting for transfers between devices, body(): lax.psum_scatter(lax.dot_general(state_rows, grad_rows, (((0,), (0,)), ((...  617 us
    unnamed x7, waiting for transfers between devices  78.8 us
    all_gather x4, blocking collectives, over_axes(): pieces = lax.all_gather(x, axis)  38.9 us
    unnamed x4, blocking collectives  29.4 us
  transfers between devices with their start and end apart: 6, of which 3 were waited for; matrix products, arithmetic and copies ran while one was open for 7% of the time, Pallas kernels for 0%

profile of v1, /device:TPU:1, one launch (start us, length us, event | category | flops | bytes accessed | tf_op | source)
XLA Modules:
  0.0 884.3 jit_solution(9101328733941864550)
XLA Ops:
  8.0 1.4 broadcast_in_dim.22
  9.4 1.2 broadcast_in_dim.23
  10.7 11.9 %all-to-all-start = ((bf16[128,4,1024]{2,1,0:T(4,128)(2,1)}), bf16[128,4,1024]{2,1,0:T(4,128)(2,1)}, u32[]{:S(2)}, u32[]{:S(2)}) async-start(bf16[128,4,1024]{2,1,0:T(4,128)(2,1)} %bitcast.67), calls=%async_computation | async-start | bytes 2097152 | tf_op jit(solution)/shard_map/all_to_all | solution.py:92
  23.3 0.6 dynamic-slice.2
  24.5 4.0 copy.17
  28.5 0.7 reduce_max.28
  29.5 0.7 dynamic-slice_reduce_fusion
  30.2 0.9 fusion.1
  31.1 5.9 copy.18
  37.7 1.4 dynamic-update-slice
  39.1 5.7 multiply_convert_fusion
  44.8 6.1 all-to-all-start.1
  50.9 2.3 gather_fusion
  53.6 6.4 fusion.23
  59.9 0.7 exponential_reduce_fusion
  60.6 3.0 multiply_reduce_fusion
  64.3 0.9 dynamic-update-slice.8
  65.2 3.7 convert_reduce_fusion
  69.8 3.5 all-reduce.15
  73.9 0.6 copy-done.2
  75.9 37.9 %all-reduce.20.cloned.1.call-done = f32[20000]{0:T(1024)} async-done(((f32[20000]{0:T(1024)}), f32[20000]{0:T(1024)}) %all-reduce.20.cloned.1.call-update) | async-done | bytes 80016
  113.8 1.0 reshape.132
  115.3 0.6 copy-done.3
  117.2 40.9 %all-reduce.22.cloned.1.call-done = f32[20000]{0:T(1024)} async-done(((f32[20000]{0:T(1024)}), f32[20000]{0:T(1024)}) %all-reduce.22.cloned.1.call-update) | async-done | bytes 80016
  158.1 1.0 reshape.133
  159.7 0.6 copy-done.4
  160.4 9.9 %fusion.19 = f32[1024,5000]{1,0:T(8,128)} fusion(bf16[128,5000]{0,1:T(8,128)(2,1)} %get-tuple-element.16, bf16[128,1024]{1,0:T(8,128)(2,1)S(1)} %gather_fusion, f32[1024]{0:T(1024)S(1)} %copy-done.5, f32[128]{0:T(128)S(1)} %add_rsqrt_fusion, f32[128]{0:T(128)S(1)} %broadcast_multiply_fusion.3), kind=kOutput, calls=%fused_computation.58 | convolution fusion | flops 1311375360 | bytes 22027264 | tf_op jit(solution)/shard_map/dot_general | solution.py:105
  170.3 0.6 reduce_sum.261
  171.5 1.4 dynamic-update-slice.9
  172.9 1.4 dynamic-update-slice.1
  174.3 8.7 all-reduce.14
  183.0 0.6 reduce_sum.262
  184.2 1.4 dynamic-update-slice.10
  185.6 1.4 dynamic-update-slice.2
  187.0 8.2 all-reduce.13
  195.2 0.6 reduce_sum.263
  196.4 1.4 dynamic-update-slice.11
  197.8 1.4 dynamic-update-slice.3
  199.2 9.0 %all-reduce.12 = (f32[4]{0:T(128)S(1)}, f32[4]{0:T(128)S(1)}) all-reduce(f32[4]{0:T(128)S(1)} %dynamic-update-slice.3, f32[4]{0:T(128)S(1)} %dynamic-update-slice.11), channel_id=1, replica_groups=mesh['teach'=2,'dp_0'=4,'dp_1'=4,'dp_2'=4] {'dp_2'}, use_global_device_ids=true, to_apply=%add.3 | all-reduce | flops 8 | bytes 64
  208.2 5.6 fusion.4
  213.8 9.1 %all-gather = f32[2048]{0:T(1024)S(1)} all-gather(f32[1024]{0:T(1024)S(1)} %fusion.4), channel_id=2, replica_groups=mesh['teach'=2,'dp_0'=4,'dp_1'=4,'dp_2'=4] {'teach'}, dimensions={0}, use_global_device_ids=true | all-gather | bytes 12288 | tf_op jit(solution)/shard_map/all_gather | solution.py:15
  222.9 9.8 %all-gather.1 = f32[4096]{0:T(1024)S(1)} all-gather(f32[1024]{0:T(1024)S(1)} %reduce_sum.251), channel_id=3, replica_groups=mesh['teach'=2,'dp_0'=4,'dp_1'=4,'dp_2'=4] {'dp_0'}, dimensions={0}, use_global_device_ids=true | all-gather | bytes 20480 | tf_op jit(solution)/shard_map/all_gather | solution.py:15
  232.7 10.0 %all-gather.2 = f32[4096]{0:T(1024)S(1)} all-gather(f32[1024]{0:T(1024)S(1)} %reduce_sum.252), channel_id=4, replica_groups=mesh['teach'=2,'dp_0'=4,'dp_1'=4,'dp_2'=4] {'dp_1'}, dimensions={0}, use_global_device_ids=true | all-gather | bytes 20480 | tf_op jit(solution)/shard_map/all_gather | solution.py:15
  242.7 10.1 %all-gather.3 = f32[4096]{0:T(1024)S(1)} all-gather(f32[1024]{0:T(1024)S(1)} %reduce_sum.253), channel_id=5, replica_groups=mesh['teach'=2,'dp_0'=4,'dp_1'=4,'dp_2'=4] {'dp_2'}, dimensions={0}, use_global_device_ids=true | all-gather | bytes 20480 | tf_op jit(solution)/shard_map/all_gather | solution.py:15
  256.0 1.0 reshape.134
  257.0 0.6 broadcast_multiply_fusion.1
  257.7 616.8 %reduce-scatter.2.cloned.1.call-done = f32[8,5000]{1,0:T(8,128)} async-done(((f32[1024,5000]{1,0:T(8,128)}), f32[8,5000]{1,0:T(8,128)}) %reduce-scatter.2.cloned.1.call-update) | async-done | bytes 160016 | tf_op jit(solution)/shard_map/reduce_scatter | solution.py:104
  874.4 1.6 broadcast_multiply_fusion
  (86 shorter events, 8.4 us)
Async XLA Ops:
  8.0 15.3 %copy-start.13 = (u32[128]{0:T(128)S(1)}, u32[128]{0:T(128)}, u32[]{:S(2)}) copy-start(u32[128]{0:T(128)} %constant.103) | copy-start | bytes 1540
  8.0 15.9 %copy-start.12 = (u32[128]{0:T(128)S(1)}, u32[128]{0:T(128)}, u32[]{:S(2)}) copy-start(u32[128]{0:T(128)} %constant.98) | copy-start | bytes 1540
  8.0 16.5 %copy-start = (bf16[1,256,5000]{1,2,0:T(8,128)(2,1)S(1)}, bf16[1,256,5000]{1,2,0:T(8,128)(2,1)}, u32[]{:S(2)}) copy-start(bf16[1,256,5000]{1,2,0:T(8,128)(2,1)} %param.9) | copy-start | bytes 7680004
  10.7 34.1 %all-to-all-start = ((bf16[128,4,1024]{2,1,0:T(4,128)(2,1)}), bf16[128,4,1024]{2,1,0:T(4,128)(2,1)}, u32[]{:S(2)}, u32[]{:S(2)}) async-start(bf16[128,4,1024]{2,1,0:T(4,128)(2,1)} %bitcast.67), calls=%async_computation | async-start | bytes 2097152 | tf_op jit(solution)/shard_map/all_to_all | solution.py:92
  28.5 0.7 copy-start.8
  28.5 0.7 copy-start.9
  31.1 8.0 copy-start.7
  44.8 15.9 %all-to-all-start.1 = ((bf16[2,128,5000]{1,2,0:T(8,128)(2,1)}), bf16[2,128,5000]{1,2,0:T(8,128)(2,1)}, u32[]{:S(2)}, u32[]{:S(2)}) async-start(bf16[2,128,5000]{1,2,0:T(8,128)(2,1)} %multiply_convert_fusion), calls=%async_computation.1 | async-start | bytes 5120000 | tf_op jit(solution)/shard_map/all_to_all | solution.py:85
  50.9 2.7 copy-start.5
  50.9 2.7 copy-start.6
  50.9 62.9 %all-reduce.20.cloned.1.call-start = ((), (), s32[]{:S(2)}) async-start(), calls=%async_computation.4 | async-start | bytes 163840
  65.1 9.5 %copy-start.11 = (u32[128]{0:T(128)S(1)}, u32[128]{0:T(128)}, u32[]{:S(2)}) copy-start(u32[128]{0:T(128)} %constant.108) | copy-start | bytes 1540
  65.2 50.9 %copy-start.10 = (u32[128]{0:T(128)S(1)}, u32[128]{0:T(128)}, u32[]{:S(2)}) copy-start(u32[128]{0:T(128)} %constant.113) | copy-start | bytes 1540
  73.9 0.6 copy-start.2
  74.6 83.5 %all-reduce.22.cloned.1.call-start = ((), (), s32[]{:S(2)}) async-start(), calls=%async_computation.5 | async-start | bytes 163840
  115.3 0.6 copy-start.3
  116.0 140.0 %all-reduce.24.cloned.1.call-start = ((), (), s32[]{:S(2)}) async-start(), calls=%async_computation.6 | async-start | bytes 163840
  159.7 0.6 copy-start.4
  160.3 714.1 %reduce-scatter.2.cloned.1.call-start = ((), (), s32[]{:S(2)}) async-start(), calls=%async_computation.3 | async-start | bytes 21135360 | tf_op jit(solution)/shard_map/reduce_scatter | solution.py:104
  170.3 37.8 %copy-start.1 = (bf16[128,5000]{0,1:T(8,128)(2,1)S(1)}, bf16[128,5000]{0,1:T(8,128)(2,1)}, u32[]{:S(2)}) copy-start(bf16[128,5000]{0,1:T(8,128)(2,1)} %get-tuple-element.16) | copy-start | bytes 3840004
Sparse Core Ops, SparseCore 0:
  74.7 39.0 all-reduce.19
  116.7 41.4 all-reduce.21
  161.0 41.9 all-reduce.23
Sparse Core Ops, SparseCore 1:
  170.4 703.9 reduce-scatter.1
